TPU v7x, 32 devices: a whole 2x2x4 slice. The times are simulated.
32 devices in a mesh: node: 16 (over z, y, x), hand: 2 (over core).
Axes of the slice: x: 2, y: 2, z: 4, core: 2. Of those that a mesh axis runs over, the one named last changes fastest.
Arguments:
- ranges: bfloat16 [512, 128, 1326], P('node', None, 'hand'), may hold values from 0.00019931793 to 0.0039978027
- strengths: int32 [512, 1326], P('node'), may hold values from 0 to 399
- live_hands: int32 [512, 1326], P('node'), may hold values 0 or 1
- pot_sizes: float32 [512, 128], P('node'), may hold values from 1 to 16
- action_counts: int32 [512], P('node'), may hold values from 1 to 8
- parents: int32 [512], P('node'), may hold values from 0 to 63
- turn_counts: int32 [16], replicated, may hold values from 1 to 4
- root_reach: float32 [16, 2, 1326], P(None, None, 'hand'), may hold values from 0.01 to 1
Outputs:
- turn_values: float32 [16, 2, 1326], P('node', None, 'hand')
- exploitability: float32 [], replicated
All inputs are finite; a program needn't handle non-finite values. No bound on the sum of `live_hands` on one device may be relied on, other than what follows from the above.
Results may differ from a plain program's by a relative error of at most 0.0003.
Values may be sent and summed in bfloat16 or wider, within the bound.
A program may use at most 128 MiB of HBM per device.

v0:
```python
import jax
import jax.numpy as jnp
import numpy as np
from jax import lax
from jax.sharding import PartitionSpec as P

ACT = 8
GROUPS = 8
TACT = 4


def card_pairs(wanted):
    first_list = []
    second_list = []
    for lower_card in range(52):
        for upper_card in range(lower_card + 1, 52):
            first_list.append(lower_card)
            second_list.append(upper_card)
    return (
        jnp.asarray(np.array(first_list[:wanted], dtype=np.int32)),
        jnp.asarray(np.array(second_list[:wanted], dtype=np.int32)),
    )


def pair_compat(row_first, row_second, col_first, col_second):
    shared = (row_first[:, None] == col_first[None, :]) | (
        row_first[:, None] == col_second[None, :]
    )
    shared = (
        shared
        | (row_second[:, None] == col_first[None, :])
        | (row_second[:, None] == col_second[None, :])
    )
    return jnp.where(shared, 0.0, 1.0).astype(jnp.float32)


def showdown_block(compat, packed):
    left_strength, left_live, right_strength, right_live, reach_block = packed
    signs = jnp.sign((left_strength[:, :, None] - right_strength[:, None, :]).astype(jnp.float32))
    matrix = (signs * compat[None] * left_live[:, :, None] * right_live[:, None, :]).astype(
        jnp.bfloat16
    )
    return jnp.einsum("nij,nlj->nli", matrix, reach_block, preferred_element_type=jnp.float32)


def river_from(raw_values, pots, legal):
    count = raw_values.shape[0]
    width = raw_values.shape[2]
    values = (raw_values * pots[:, :, None]).reshape(count, 2, GROUPS, ACT, width)
    usable = jnp.arange(ACT)[None, :] < legal[:, None]
    return jnp.where(usable[:, None, None, :, None], values, -1e30).max(axis=3).sum(axis=2)


def turn_best(sums, legal):
    hand_half = sums.shape[1] // 2
    shaped = sums.reshape(-1, TACT, 2, hand_half)
    usable = jnp.arange(TACT)[None, :] < legal[:, None]
    return jnp.where(usable[:, :, None, None], shaped, -1e30).max(axis=1)


def local(
    ranges, strengths, live_hands, pot_sizes, action_counts, parents, turn_counts, root_reach
):
    node_count, line_cols, hand_half = ranges.shape
    hands_all = strengths.shape[1]
    hand_start = lax.axis_index("hand") * hand_half
    first_card, second_card = card_pairs(hands_all)
    live_all = live_hands.astype(jnp.float32)
    blocks = node_count // 4

    def grouped(array):
        return array.reshape((blocks, 4) + array.shape[1:])

    row_first = lax.dynamic_slice_in_dim(first_card, hand_start, hand_half, 0)
    row_second = lax.dynamic_slice_in_dim(second_card, hand_start, hand_half, 0)
    row_strength = lax.dynamic_slice_in_dim(strengths, hand_start, hand_half, 1)
    row_live = lax.dynamic_slice_in_dim(live_all, hand_start, hand_half, 1)
    compat = pair_compat(row_first, row_second, first_card, second_card)

    def one_block(packed):
        return showdown_block(compat, packed)

    added = lax.map(
        one_block,
        (
            grouped(row_strength),
            grouped(row_live),
            grouped(strengths),
            grouped(live_all),
            grouped(lax.all_gather(ranges, "hand", axis=2, tiled=True)),
        ),
    )
    raw_values = added.reshape(jnp.zeros((node_count, line_cols, hand_half), jnp.float32).shape)
    river_best = river_from(raw_values, pot_sizes, action_counts)
    flat_best = river_best.reshape(node_count, 2 * hand_half)
    turns_all = turn_counts.shape[0]
    turns_mine = turns_all // lax.axis_size("node")
    turn_start = lax.axis_index("node") * turns_mine
    parents_all = turns_all * TACT
    onehot = (parents[None, :] == jnp.arange(parents_all, dtype=jnp.int32)[:, None]).astype(
        jnp.float32
    )
    local_sums = jnp.dot(onehot, flat_best, precision=lax.Precision.HIGHEST)
    totals = lax.psum(local_sums, "node")
    values_all = turn_best(totals, turn_counts)
    exploitability = lax.psum(jnp.sum(root_reach * values_all), "hand")
    turn_values = lax.dynamic_slice_in_dim(values_all, turn_start, turns_mine, 0)
    return (turn_values, exploitability)


def solution(mesh):
    in_specs = (
        P("node", None, "hand"),
        P("node", None),
        P("node", None),
        P("node", None),
        P("node"),
        P("node"),
        P(),
        P(None, None, "hand"),
    )
    out_specs = (P("node", None, "hand"), P())
    return jax.shard_map(local, mesh=mesh, in_specs=in_specs, out_specs=out_specs, check_vma=False)
```

profile of v0, /device:TPU:0, one launch (start us, length us, event | category | flops | bytes accessed | tf_op | source)
XLA Modules:
  0.0 278.7 jit_solution(3800787151186367840)
XLA Ops:
  7.2 0.0 all-gather.2.cloned.1.call-start
  7.2 0.7 all-gather.2.cloned.1.call-update
  7.9 0.0 all-reduce.2.cloned.1.call-start
  8.0 0.9 convert_element_type.10
  8.9 0.1 reshape.92
  9.0 0.1 constant_dynamic-slice_fusion.2
  9.1 1.0 reshape.90
  10.1 1.0 constant_dynamic-slice_fusion.3
  11.1 0.8 dynamic_slice.36
  11.9 0.8 dynamic_slice.37
  12.7 0.8 copy.23
  13.5 0.2 copy.24
  13.7 0.7 iota_compare_fusion.2
  14.4 20.9 %all-gather.2.cloned.1.call-done = bf16[32,128,1326]{1,0,2:T(8,128)(2,1)} async-done(((bf16[32,128,663]{1,0,2:T(8,128)(2,1)}), bf16[32,128,1326]{1,0,2:T(8,128)(2,1)}) %all-gather.2.cloned.1.call-update) | async-done | bytes 10862608 | tf_op jit(solution)/shard_map/all_gather | solution.py:90
  35.3 89.9 %while.11 = (s32[]{:T(128)}, f32[8,4,128,663]{2,3,1,0:T(8,128)}, bf16[8,4,128,1326]{2,1,0,3:T(4,128)(2,1)}, s32[8,4,663]{2,1,0:T(4,128)S(1)}, s32[8,4,1326]{2,1,...) while((s32[]{:T(128)}, f32[8,4,128,663]{2,3,1,0:T(8,128)}, ...), condition=%wide.region_1.2_spmd.clone, body=%wide.region_0.1_spmd.clone.sunk | while | flops 931886272 | bytes 12673953 | solution.py:83
  35.3 1.6 constant_dynamic-slice_fusion.5
  37.0 2.2 or_select_fusion.2
  39.2 7.4 %fusion.9 = f32[8,4,128,663]{2,3,1,0:T(8,128)} fusion(f32[8,4,128,663]{2,3,1,0:T(8,128)} %get-tuple-element.197, s32[]{:T(128)} %get-tuple-element.196, f32[4,1326]{1,0:T(4,128)S(1)} %dynamic-slice_bitcast_fusion.8, f32[4,663]{1,0:T(4,128)S(1)} %dynamic-slice_bitcast_fusion.9, f32[663,1326]{1,0:T(8,128)S(1)} %or_select_fusion.2, ...), kind=kOutput, calls=%fused_computation.5.clone.1 | convolution fusion | flops 924853184 | bytes 6298408 | tf_op jit(solution)/shard_map/while/body/eval_jaxpr/nij,nlj->nli/dot_general | solution.py:43
  46.6 1.6 constant_dynamic-slice_fusion.5
  48.3 2.2 or_select_fusion.2
  50.5 7.3 %fusion.9 = f32[8,4,128,663]{2,3,1,0:T(8,128)} fusion(f32[8,4,128,663]{2,3,1,0:T(8,128)} %get-tuple-element.197, s32[]{:T(128)} %get-tuple-element.196, f32[4,1326]{1,0:T(4,128)S(1)} %dynamic-slice_bitcast_fusion.8, f32[4,663]{1,0:T(4,128)S(1)} %dynamic-slice_bitcast_fusion.9, f32[663,1326]{1,0:T(8,128)S(1)} %or_select_fusion.2, ...), kind=kOutput, calls=%fused_computation.5.clone.1 | convolution fusion | flops 924853184 | bytes 6298408 | tf_op jit(solution)/shard_map/while/body/eval_jaxpr/nij,nlj->nli/dot_general | solution.py:43
  57.8 1.6 constant_dynamic-slice_fusion.5
  59.5 2.2 or_select_fusion.2
  61.7 7.3 %fusion.9 = f32[8,4,128,663]{2,3,1,0:T(8,128)} fusion(f32[8,4,128,663]{2,3,1,0:T(8,128)} %get-tuple-element.197, s32[]{:T(128)} %get-tuple-element.196, f32[4,1326]{1,0:T(4,128)S(1)} %dynamic-slice_bitcast_fusion.8, f32[4,663]{1,0:T(4,128)S(1)} %dynamic-slice_bitcast_fusion.9, f32[663,1326]{1,0:T(8,128)S(1)} %or_select_fusion.2, ...), kind=kOutput, calls=%fused_computation.5.clone.1 | convolution fusion | flops 924853184 | bytes 6298408 | tf_op jit(solution)/shard_map/while/body/eval_jaxpr/nij,nlj->nli/dot_general | solution.py:43
  69.0 1.6 constant_dynamic-slice_fusion.5
  70.7 2.2 or_select_fusion.2
  73.0 7.3 %fusion.9 = f32[8,4,128,663]{2,3,1,0:T(8,128)} fusion(f32[8,4,128,663]{2,3,1,0:T(8,128)} %get-tuple-element.197, s32[]{:T(128)} %get-tuple-element.196, f32[4,1326]{1,0:T(4,128)S(1)} %dynamic-slice_bitcast_fusion.8, f32[4,663]{1,0:T(4,128)S(1)} %dynamic-slice_bitcast_fusion.9, f32[663,1326]{1,0:T(8,128)S(1)} %or_select_fusion.2, ...), kind=kOutput, calls=%fused_computation.5.clone.1 | convolution fusion | flops 924853184 | bytes 6298408 | tf_op jit(solution)/shard_map/while/body/eval_jaxpr/nij,nlj->nli/dot_general | solution.py:43
  80.2 1.6 constant_dynamic-slice_fusion.5
  81.9 2.2 or_select_fusion.2
  84.2 7.3 %fusion.9 = f32[8,4,128,663]{2,3,1,0:T(8,128)} fusion(f32[8,4,128,663]{2,3,1,0:T(8,128)} %get-tuple-element.197, s32[]{:T(128)} %get-tuple-element.196, f32[4,1326]{1,0:T(4,128)S(1)} %dynamic-slice_bitcast_fusion.8, f32[4,663]{1,0:T(4,128)S(1)} %dynamic-slice_bitcast_fusion.9, f32[663,1326]{1,0:T(8,128)S(1)} %or_select_fusion.2, ...), kind=kOutput, calls=%fused_computation.5.clone.1 | convolution fusion | flops 924853184 | bytes 6298408 | tf_op jit(solution)/shard_map/while/body/eval_jaxpr/nij,nlj->nli/dot_general | solution.py:43
  91.5 1.6 constant_dynamic-slice_fusion.5
  93.2 2.2 or_select_fusion.2
  95.4 7.3 %fusion.9 = f32[8,4,128,663]{2,3,1,0:T(8,128)} fusion(f32[8,4,128,663]{2,3,1,0:T(8,128)} %get-tuple-element.197, s32[]{:T(128)} %get-tuple-element.196, f32[4,1326]{1,0:T(4,128)S(1)} %dynamic-slice_bitcast_fusion.8, f32[4,663]{1,0:T(4,128)S(1)} %dynamic-slice_bitcast_fusion.9, f32[663,1326]{1,0:T(8,128)S(1)} %or_select_fusion.2, ...), kind=kOutput, calls=%fused_computation.5.clone.1 | convolution fusion | flops 924853184 | bytes 6298408 | tf_op jit(solution)/shard_map/while/body/eval_jaxpr/nij,nlj->nli/dot_general | solution.py:43
  102.7 1.6 constant_dynamic-slice_fusion.5
  104.4 2.2 or_select_fusion.2
  106.7 7.3 %fusion.9 = f32[8,4,128,663]{2,3,1,0:T(8,128)} fusion(f32[8,4,128,663]{2,3,1,0:T(8,128)} %get-tuple-element.197, s32[]{:T(128)} %get-tuple-element.196, f32[4,1326]{1,0:T(4,128)S(1)} %dynamic-slice_bitcast_fusion.8, f32[4,663]{1,0:T(4,128)S(1)} %dynamic-slice_bitcast_fusion.9, f32[663,1326]{1,0:T(8,128)S(1)} %or_select_fusion.2, ...), kind=kOutput, calls=%fused_computation.5.clone.1 | convolution fusion | flops 924853184 | bytes 6298408 | tf_op jit(solution)/shard_map/while/body/eval_jaxpr/nij,nlj->nli/dot_general | solution.py:43
  113.9 1.6 constant_dynamic-slice_fusion.5
  115.6 2.2 or_select_fusion.2
  117.9 7.3 %fusion.9 = f32[8,4,128,663]{2,3,1,0:T(8,128)} fusion(f32[8,4,128,663]{2,3,1,0:T(8,128)} %get-tuple-element.197, s32[]{:T(128)} %get-tuple-element.196, f32[4,1326]{1,0:T(4,128)S(1)} %dynamic-slice_bitcast_fusion.8, f32[4,663]{1,0:T(4,128)S(1)} %dynamic-slice_bitcast_fusion.9, f32[663,1326]{1,0:T(8,128)S(1)} %or_select_fusion.2, ...), kind=kOutput, calls=%fused_computation.5.clone.1 | convolution fusion | flops 924853184 | bytes 6298408 | tf_op jit(solution)/shard_map/while/body/eval_jaxpr/nij,nlj->nli/dot_general | solution.py:43
  125.2 12.0 %copy.22 = f32[8,4,128,663]{3,2,1,0:T(8,128)} copy(f32[8,4,128,663]{2,3,1,0:T(8,128)} %get-tuple-element.44) | data formatting | bytes 21725184 | tf_op jit(solution)/shard_map/while | solution.py:83
  137.1 0.0 copy-start.1
  137.1 0.0 copy-start.2
  137.1 0.0 copy-start
  137.1 16.8 %select_reduce_fusion = f32[32,2,8,663]{3,2,1,0:T(8,128)S(1)} fusion(f32[32,2,8,8,663]{4,3,2,1,0:T(8,128)} %bitcast.31, f32[32,2,8,8]{3,2,1,0:T(8,128)S(1)} %copy.24, pred[32,8]{1,0:T(8,128)(4,1)S(1)} %iota_compare_fusion.2), kind=kLoop, calls=%fused_computation.12 | loop fusion | flops 7807488 | bytes 12237056 | tf_op jit(solution)/shard_map/reduce_max | solution.py:51
  153.9 0.5 reduce_sum.18
  154.4 0.2 reshape.94
  154.6 0.0 copy-done.1
  154.6 0.3 fusion.5
  154.9 1.1 reshape.95
  156.0 0.0 all-reduce.2.cloned.1.call-update
  156.1 0.0 copy-done.2
  156.1 0.1 iota_compare_fusion.3
  156.2 109.9 %all-reduce.2.cloned.1.call-done = f32[16,4,2,663]{3,2,1,0:T(2,128)} async-done(((f32[16,4,2,663]{3,2,1,0:T(2,128)}), f32[16,4,2,663]{3,2,1,0:T(2,128)}) %all-reduce.2.cloned.1.call-update) | async-done | bytes 339472 | tf_op jit(solution)/shard_map/psum | solution.py:104
  266.1 1.4 select_reduce_fusion.1
  267.5 0.0 copy-done
  267.5 0.7 multiply_reduce_fusion
  268.2 0.6 constant_dynamic-slice_fusion.1
  268.8 3.1 %psum.15 = f32[]{:T(128)} all-reduce(f32[]{:T(128)} %multiply_reduce_fusion), channel_id=1, replica_groups=mesh['node'=16,'hand'=2] {'hand'}, use_global_device_ids=true, to_apply=%region_7.8 | all-reduce | flops 1 | bytes 8 | tf_op jit(solution)/shard_map/psum | solution.py:106
  (35 shorter events, 0.4 us)
Async XLA Ops:
  7.2 28.1 %all-gather.2.cloned.1.call-start = ((), (), s32[]{:S(2)}) async-start(), calls=%async_computation | async-start | bytes 16293888 | tf_op jit(solution)/shard_map/all_gather | solution.py:90
  7.9 258.2 %all-reduce.2.cloned.1.call-start = ((), (), s32[]{:S(2)}) async-start(), calls=%async_computation.1 | async-start | bytes 786432 | tf_op jit(solution)/shard_map/psum | solution.py:104
  137.1 17.5 %copy-start.1 = (s32[32]{0:T(128)S(1)}, s32[32]{0:T(128)}, u32[]{:S(2)}) copy-start(s32[32]{0:T(128)} %param.17) | copy-start | bytes 388
  137.1 18.9 %copy-start.2 = (s32[16]{0:T(128)S(1)}, s32[16]{0:T(128)}, u32[]{:S(2)}) copy-start(s32[16]{0:T(128)} %param.18) | copy-start | bytes 196
  137.1 130.4 %copy-start = (f32[16,2,663]{2,1,0:T(2,128)S(1)}, f32[16,2,663]{2,1,0:T(2,128)}, u32[]{:S(2)}) copy-start(f32[16,2,663]{2,1,0:T(2,128)} %param.19) | copy-start | bytes 254596
Sparse Core Ops, SparseCore 0:
  9.5 25.7 all-gather.1
  156.2 109.8 all-reduce.1
where the time goes:
time: 280 us; the launch traced here: 279 us
  waiting for transfers between devices  132 us (47%)
  matrix products  58.7 us (21%)
  other arithmetic  39.1 us (14%)
  local copies, waits for them, and re-layouts  31.7 us (11%)
  between operations  14.2 us (5%)
  blocking collectives  3.08 us (1%)
    psum x1, waiting for transfers between devices, local(): totals = lax.psum(local_sums, 'node')  110 us
    dot_general x8, matrix products, showdown_block(): jnp.einsum('nij,nlj->nli', matrix, reach_block, preferred_element_type=jn...  58.4 us
    all_gather x1, waiting for transfers between devices, local(): lax.all_gather(ranges, 'hand', axis=2, tiled=True)  20.9 us
    select_n x8, other arithmetic, pair_compat(): return jnp.where(shared, 0.0, 1.0).astype(jnp.float32)  17.9 us
    reduce_max x1, other arithmetic, river_from(): jnp.where(usable[:, None, None, :, None], values, -1e+30).max(axis=3)  16.8 us
    dynamic_slice x8, local copies, waits for them, and re-layouts, local(): lax.map(one_block, (grouped(row_strength), grouped(row_live), grouped(str...  12.8 us
    while x1, local copies, waits for them, and re-layouts, local(): lax.map(one_block, (grouped(row_strength), grouped(row_live), grouped(str...  12 us
  transfers between devices with their start and end apart: 2, of which 2 were waited for; matrix products, arithmetic and copies ran while one was open for 2% of the time, Pallas kernels for 0%

commit v1 on v0

--- a/solution.py
+++ b/solution.py
@@ -101,7 +101,7 @@
         jnp.float32
     )
     local_sums = jnp.dot(onehot, flat_best, precision=lax.Precision.HIGHEST)
-    totals = lax.psum(local_sums, "node")
+    totals = jnp.sum(lax.all_gather(local_sums, "node"), axis=0)
     values_all = turn_best(totals, turn_counts)
     exploitability = lax.psum(jnp.sum(root_reach * values_all), "hand")
     turn_values = lax.dynamic_slice_in_dim(values_all, turn_start, turns_mine, 0)

time: 280 us -> 262 us (0.936)
  waiting for transfers between devices: 132 us -> 112 us
    psum x1 -> x0, waiting for transfers between devices: 110 us -> none  [local(): totals = lax.psum(local_sums, 'node')]
    all_gather x0 -> x1, waiting for transfers between devices: none -> 90 us  [local(): totals = jnp.sum(lax.all_gather(local_sums, 'node'), axis=0)]
    reduce_sum x0 -> x1, other arithmetic: none -> 2.95 us  [local(): totals = jnp.sum(lax.all_gather(local_sums, 'node'), axis=0)]
where the time goes in v1:
time: 262 us; the launch traced here: 261 us
  waiting for transfers between devices  112 us (43%)
  matrix products  59.4 us (23%)
  other arithmetic  40.9 us (16%)
  local copies, waits for them, and re-layouts  31 us (12%)
  between operations  14.2 us (5%)
  blocking collectives  3.08 us (1%)
    all_gather x1, waiting for transfers between devices, local(): totals = jnp.sum(lax.all_gather(local_sums, 'node'), axis=0)  90 us
    dot_general x8, matrix products, showdown_block(): jnp.einsum('nij,nlj->nli', matrix, reach_block, preferred_element_type=jn...  58.4 us
    all_gather x1, waiting for transfers between devices, local(): lax.all_gather(ranges, 'hand', axis=2, tiled=True)  20.9 us
    select_n x8, other arithmetic, pair_compat(): return jnp.where(shared, 0.0, 1.0).astype(jnp.float32)  17.9 us
    reduce_max x1, other arithmetic, river_from(): jnp.where(usable[:, None, None, :, None], values, -1e+30).max(axis=3)  16.8 us
    dynamic_slice x8, local copies, waits for them, and re-layouts, local(): lax.map(one_block, (grouped(row_strength), grouped(row_live), grouped(str...  12.8 us
    while x1, local copies, waits for them, and re-layouts, local(): lax.map(one_block, (grouped(row_strength), grouped(row_live), grouped(str...  12 us
  transfers between devices with their start and end apart: 2, of which 2 were waited for; matrix products, arithmetic and copies ran while one was open for 2% of the time, Pallas kernels for 0%

profile of v1, /device:TPU:0, one launch (start us, length us, event | category | flops | bytes accessed | tf_op | source)
XLA Modules:
  0.0 260.6 jit_solution(15740748312715223570)
XLA Ops:
  7.2 0.0 all-gather.4.cloned.1.call-start
  7.2 0.7 all-gather.4.cloned.1.call-update
  7.9 0.0 all-gather.6.cloned.1.call-start
  8.0 0.9 convert_element_type.10
  8.9 0.1 reshape.92
  9.0 0.1 constant_dynamic-slice_fusion.2
  9.1 1.0 reshape.90
  10.1 1.0 constant_dynamic-slice_fusion.3
  11.1 0.8 dynamic_slice.36
  11.9 0.8 dynamic_slice.37
  12.7 0.8 copy.29
  13.5 0.2 copy.30
  13.7 0.7 iota_compare_fusion.2
  14.4 20.9 %all-gather.4.cloned.1.call-done = bf16[32,128,1326]{1,0,2:T(8,128)(2,1)} async-done(((bf16[32,128,663]{1,0,2:T(8,128)(2,1)}), bf16[32,128,1326]{1,0,2:T(8,128)(2,1)}) %all-gather.4.cloned.1.call-update) | async-done | bytes 10862608 | tf_op jit(solution)/shard_map/all_gather | solution.py:90
  35.3 89.9 %while.11 = (s32[]{:T(128)}, f32[8,4,128,663]{2,3,1,0:T(8,128)}, bf16[8,4,128,1326]{2,1,0,3:T(4,128)(2,1)}, s32[8,4,663]{2,1,0:T(4,128)S(1)}, s32[8,4,1326]{2,1,...) while((s32[]{:T(128)}, f32[8,4,128,663]{2,3,1,0:T(8,128)}, ...), condition=%wide.region_1.2_spmd.clone, body=%wide.region_0.1_spmd.clone.sunk | while | flops 931886272 | bytes 12673953 | solution.py:83
  35.3 1.6 constant_dynamic-slice_fusion.5
  37.0 2.2 or_select_fusion.2
  39.2 7.3 %fusion.10 = f32[8,4,128,663]{2,3,1,0:T(8,128)} fusion(f32[8,4,128,663]{2,3,1,0:T(8,128)} %get-tuple-element.214, s32[]{:T(128)} %get-tuple-element.213, f32[4,1326]{1,0:T(4,128)S(1)} %dynamic-slice_bitcast_fusion.8, f32[4,663]{1,0:T(4,128)S(1)} %dynamic-slice_bitcast_fusion.9, f32[663,1326]{1,0:T(8,128)S(1)} %or_select_fusion.2, ...), kind=kOutput, calls=%fused_computation.5.clone.1 | convolution fusion | flops 924853184 | bytes 6298408 | tf_op jit(solution)/shard_map/while/body/eval_jaxpr/nij,nlj->nli/dot_general | solution.py:43
  46.6 1.6 constant_dynamic-slice_fusion.5
  48.3 2.2 or_select_fusion.2
  50.5 7.3 %fusion.10 = f32[8,4,128,663]{2,3,1,0:T(8,128)} fusion(f32[8,4,128,663]{2,3,1,0:T(8,128)} %get-tuple-element.214, s32[]{:T(128)} %get-tuple-element.213, f32[4,1326]{1,0:T(4,128)S(1)} %dynamic-slice_bitcast_fusion.8, f32[4,663]{1,0:T(4,128)S(1)} %dynamic-slice_bitcast_fusion.9, f32[663,1326]{1,0:T(8,128)S(1)} %or_select_fusion.2, ...), kind=kOutput, calls=%fused_computation.5.clone.1 | convolution fusion | flops 924853184 | bytes 6298408 | tf_op jit(solution)/shard_map/while/body/eval_jaxpr/nij,nlj->nli/dot_general | solution.py:43
  57.8 1.6 constant_dynamic-slice_fusion.5
  59.5 2.2 or_select_fusion.2
  61.7 7.3 %fusion.10 = f32[8,4,128,663]{2,3,1,0:T(8,128)} fusion(f32[8,4,128,663]{2,3,1,0:T(8,128)} %get-tuple-element.214, s32[]{:T(128)} %get-tuple-element.213, f32[4,1326]{1,0:T(4,128)S(1)} %dynamic-slice_bitcast_fusion.8, f32[4,663]{1,0:T(4,128)S(1)} %dynamic-slice_bitcast_fusion.9, f32[663,1326]{1,0:T(8,128)S(1)} %or_select_fusion.2, ...), kind=kOutput, calls=%fused_computation.5.clone.1 | convolution fusion | flops 924853184 | bytes 6298408 | tf_op jit(solution)/shard_map/while/body/eval_jaxpr/nij,nlj->nli/dot_general | solution.py:43
  69.0 1.6 constant_dynamic-slice_fusion.5
  70.7 2.2 or_select_fusion.2
  73.0 7.3 %fusion.10 = f32[8,4,128,663]{2,3,1,0:T(8,128)} fusion(f32[8,4,128,663]{2,3,1,0:T(8,128)} %get-tuple-element.214, s32[]{:T(128)} %get-tuple-element.213, f32[4,1326]{1,0:T(4,128)S(1)} %dynamic-slice_bitcast_fusion.8, f32[4,663]{1,0:T(4,128)S(1)} %dynamic-slice_bitcast_fusion.9, f32[663,1326]{1,0:T(8,128)S(1)} %or_select_fusion.2, ...), kind=kOutput, calls=%fused_computation.5.clone.1 | convolution fusion | flops 924853184 | bytes 6298408 | tf_op jit(solution)/shard_map/while/body/eval_jaxpr/nij,nlj->nli/dot_general | solution.py:43
  80.2 1.6 constant_dynamic-slice_fusion.5
  81.9 2.2 or_select_fusion.2
  84.2 7.3 %fusion.10 = f32[8,4,128,663]{2,3,1,0:T(8,128)} fusion(f32[8,4,128,663]{2,3,1,0:T(8,128)} %get-tuple-element.214, s32[]{:T(128)} %get-tuple-element.213, f32[4,1326]{1,0:T(4,128)S(1)} %dynamic-slice_bitcast_fusion.8, f32[4,663]{1,0:T(4,128)S(1)} %dynamic-slice_bitcast_fusion.9, f32[663,1326]{1,0:T(8,128)S(1)} %or_select_fusion.2, ...), kind=kOutput, calls=%fused_computation.5.clone.1 | convolution fusion | flops 924853184 | bytes 6298408 | tf_op jit(solution)/shard_map/while/body/eval_jaxpr/nij,nlj->nli/dot_general | solution.py:43
  91.5 1.6 constant_dynamic-slice_fusion.5
  93.2 2.2 or_select_fusion.2
  95.4 7.3 %fusion.10 = f32[8,4,128,663]{2,3,1,0:T(8,128)} fusion(f32[8,4,128,663]{2,3,1,0:T(8,128)} %get-tuple-element.214, s32[]{:T(128)} %get-tuple-element.213, f32[4,1326]{1,0:T(4,128)S(1)} %dynamic-slice_bitcast_fusion.8, f32[4,663]{1,0:T(4,128)S(1)} %dynamic-slice_bitcast_fusion.9, f32[663,1326]{1,0:T(8,128)S(1)} %or_select_fusion.2, ...), kind=kOutput, calls=%fused_computation.5.clone.1 | convolution fusion | flops 924853184 | bytes 6298408 | tf_op jit(solution)/shard_map/while/body/eval_jaxpr/nij,nlj->nli/dot_general | solution.py:43
  102.7 1.6 constant_dynamic-slice_fusion.5
  104.4 2.2 or_select_fusion.2
  106.6 7.3 %fusion.10 = f32[8,4,128,663]{2,3,1,0:T(8,128)} fusion(f32[8,4,128,663]{2,3,1,0:T(8,128)} %get-tuple-element.214, s32[]{:T(128)} %get-tuple-element.213, f32[4,1326]{1,0:T(4,128)S(1)} %dynamic-slice_bitcast_fusion.8, f32[4,663]{1,0:T(4,128)S(1)} %dynamic-slice_bitcast_fusion.9, f32[663,1326]{1,0:T(8,128)S(1)} %or_select_fusion.2, ...), kind=kOutput, calls=%fused_computation.5.clone.1 | convolution fusion | flops 924853184 | bytes 6298408 | tf_op jit(solution)/shard_map/while/body/eval_jaxpr/nij,nlj->nli/dot_general | solution.py:43
  113.9 1.6 constant_dynamic-slice_fusion.5
  115.6 2.2 or_select_fusion.2
  117.8 7.3 %fusion.10 = f32[8,4,128,663]{2,3,1,0:T(8,128)} fusion(f32[8,4,128,663]{2,3,1,0:T(8,128)} %get-tuple-element.214, s32[]{:T(128)} %get-tuple-element.213, f32[4,1326]{1,0:T(4,128)S(1)} %dynamic-slice_bitcast_fusion.8, f32[4,663]{1,0:T(4,128)S(1)} %dynamic-slice_bitcast_fusion.9, f32[663,1326]{1,0:T(8,128)S(1)} %or_select_fusion.2, ...), kind=kOutput, calls=%fused_computation.5.clone.1 | convolution fusion | flops 924853184 | bytes 6298408 | tf_op jit(solution)/shard_map/while/body/eval_jaxpr/nij,nlj->nli/dot_general | solution.py:43
  125.2 12.0 %copy.28 = f32[8,4,128,663]{3,2,1,0:T(8,128)} copy(f32[8,4,128,663]{2,3,1,0:T(8,128)} %get-tuple-element.44) | data formatting | bytes 21725184 | tf_op jit(solution)/shard_map/while | solution.py:83
  137.1 0.0 copy-start.1
  137.1 0.0 copy-start.2
  137.1 0.0 copy-start
  137.1 16.8 %select_reduce_fusion = f32[32,2,8,663]{3,2,1,0:T(8,128)S(1)} fusion(f32[32,2,8,8,663]{4,3,2,1,0:T(8,128)} %bitcast.32, f32[32,2,8,8]{3,2,1,0:T(8,128)S(1)} %copy.30, pred[32,8]{1,0:T(8,128)(4,1)S(1)} %iota_compare_fusion.2), kind=kLoop, calls=%fused_computation.12 | loop fusion | flops 7807488 | bytes 12237056 | tf_op jit(solution)/shard_map/reduce_max | solution.py:51
  153.9 0.5 reduce_sum.27
  154.4 0.2 reshape.94
  154.6 0.0 copy-done.1
  154.6 1.0 fusion.6
  155.6 0.0 all-gather.6.cloned.1.call-update
  155.6 0.0 copy-done.2
  155.7 0.1 iota_compare_fusion.3
  155.7 90.0 %all-gather.6.cloned.1.call-done = f32[1024,1326]{1,0:T(8,128)} async-done(((f32[64,1326]{1,0:T(8,128)}), f32[1024,1326]{1,0:T(8,128)}) %all-gather.6.cloned.1.call-update) | async-done | bytes 5431312 | tf_op jit(solution)/shard_map/all_gather | solution.py:104
  245.7 3.0 %reduce_sum.28 = f32[64,1326]{1,0:T(8,128)S(1)} reduce(f32[16,64,1326]{2,1,0:T(8,128)} %bitcast.33, f32[]{:T(128)} %constant.19.clone.1), dimensions={0}, to_apply=%region_4.5 | reduce | flops 1272960 | bytes 5770756 | tf_op jit(solution)/shard_map/reduce_sum | solution.py:104
  248.7 0.4 reshape.95
  249.1 0.4 select_reduce_fusion.1
  249.5 0.0 copy-done
  249.5 0.6 fusion.5
  250.1 0.6 copy.33
  250.7 3.1 %psum.7 = f32[]{:T(128)} all-reduce(f32[]{:T(128)} %get-tuple-element.132), channel_id=1, replica_groups=mesh['node'=16,'hand'=2] {'hand'}, use_global_device_ids=true, to_apply=%region_7.8 | all-reduce | flops 1 | bytes 8 | tf_op jit(solution)/shard_map/psum | solution.py:106
  (36 shorter events, 0.4 us)
Async XLA Ops:
  7.2 28.1 %all-gather.4.cloned.1.call-start = ((), (), s32[]{:S(2)}) async-start(), calls=%async_computation | async-start | bytes 16293888 | tf_op jit(solution)/shard_map/all_gather | solution.py:90
  7.9 237.8 %all-gather.6.cloned.1.call-start = ((), (), s32[]{:S(2)}) async-start(), calls=%async_computation.1 | async-start | bytes 6127616 | tf_op jit(solution)/shard_map/all_gather | solution.py:104
  137.1 17.5 %copy-start.1 = (s32[32]{0:T(128)S(1)}, s32[32]{0:T(128)}, u32[]{:S(2)}) copy-start(s32[32]{0:T(128)} %param.17) | copy-start | bytes 388
  137.1 18.5 %copy-start.2 = (s32[16]{0:T(128)S(1)}, s32[16]{0:T(128)}, u32[]{:S(2)}) copy-start(s32[16]{0:T(128)} %param.18) | copy-start | bytes 196
  137.1 112.4 %copy-start = (f32[16,2,663]{2,1,0:T(2,128)S(1)}, f32[16,2,663]{2,1,0:T(2,128)}, u32[]{:S(2)}) copy-start(f32[16,2,663]{2,1,0:T(2,128)} %param.19) | copy-start | bytes 254596
Sparse Core Ops, SparseCore 0:
  9.5 25.7 all-gather.3
  155.8 89.9 all-gather.5
